TPU v7x, 128 devices: a whole 4x4x4 slice. The times are simulated.
128 devices in a mesh: dp: 32 (over z, y, core), tensor: 4 (over x).
Axes of the slice: x: 4, y: 4, z: 4, core: 2. Of those that a mesh axis runs over, the one named last changes fastest.
Arguments:
- sampled_earlier_tokens: int32 [128, 169], P('dp'), may hold values from 0 to 4095
- quantizer_vectors: float32 [4096, 32], replicated, may hold values from -6 to 6
- summed_latent_canvas: float32 [128, 256, 32], P('dp'), may hold values from -6 to 6
- latent_lift_matrix: float32 [32, 1536], replicated, may hold values from -1 to 1
- location_tier_offset: float32 [256, 1536], replicated, may hold values from -3 to 3
- adaptive_norm_factors: float32 [1, 128, 6, 1536], P(None, 'dp'), may hold values from -3 to 3
- logit_sharpness: float32 [1, 16], P(None, 'tensor'), may hold values from 2 to 240, as said below
- probe_match_content_matrix: bfloat16 [1, 1536, 3, 1536], P(None, 'dp', None, 'tensor'), may hold values from -1 to 1, as said below
- mixing_projection_matrix: bfloat16 [1, 1536, 1536], P(None, 'tensor', 'dp'), may hold values from -0.15625 to 0.15625
- widening_projection_matrix: bfloat16 [1, 1536, 6144], P(None, 'dp', 'tensor'), may hold values from -0.15625 to 0.15625
- narrowing_projection_matrix: bfloat16 [1, 6144, 1536], P(None, 'tensor', 'dp'), may hold values from -0.078125 to 0.078125
- cached_lower_grid_lookups: bfloat16 [1, 128, 424, 1536], P(None, 'dp', None, 'tensor'), may hold values from -6 to 6
- cached_lower_grid_payloads: bfloat16 [1, 128, 424, 1536], P(None, 'dp', None, 'tensor'), may hold values from -6 to 6
- final_norm_factors: float32 [128, 2, 1536], P('dp'), may hold values from -3 to 3
- vocabulary_logit_matrix: bfloat16 [1536, 4096], P(None, 'tensor'), may hold values from -0.15625 to 0.15625
Outputs:
- logits: bfloat16 [128, 256, 4096], P('dp', None, 'tensor')
- canvas: float32 [128, 256, 32], P('dp')
Inputs may be any that keep to these rules, and one draw needn't show every extreme that they name: `logit_sharpness`: Positive. `probe_match_content_matrix`: entries of spread about 1536 ** -0.5.
All inputs are finite; a program needn't handle non-finite values.
Results may differ from a plain program's by a relative error of at most 0.015.
Values may be sent and summed in bfloat16 or wider, within the bound.
A program may use at most 128 MiB of HBM per device.

v0:
```python
import numpy as np
import jax
import jax.numpy as jnp
from jax import lax
from jax.experimental import pallas as pl
from jax.experimental.pallas import tpu as pltpu
from jax.sharding import PartitionSpec as P

MESH = pl.DeviceIdType.MESH
BF = jnp.bfloat16
F32 = jnp.float32

D = 1536
HEADS_L = 4
HDIM = 96
LW = HEADS_L * HDIM
VOCAB = 4096
VL = 1024
CVAE = 32
SIDE = 16
PREV = 13
PREVPAD = 176
CACHE = 424
TOK = 256
HALF = 128
IMGS = 4
SH = 48
NX = 4
FLOOR = 0.1

WINDOWS = ((0, 128), (0, 256), (128, 384), (256, 384))

SPLITS = (
    ((0, 640, 384), (640, 1152, 896)),
    ((0, 768, 384), (768, 1536, 1152)),
    ((0, 768, 384), (768, 1536, 1152)),
    ((0, 768, 384), (768, 1536, 1152)),
)


def upsample_matrix():
    a = np.arange(SIDE)
    num = np.maximum((2 * a + 1) * PREV - SIDE, 0)
    low = num // (2 * SIDE)
    frac = (num % (2 * SIDE)) / (2.0 * SIDE)
    up = np.zeros((SIDE, PREV))
    up[a, low] += 1.0 - frac
    up[a, np.minimum(low + 1, PREV - 1)] += frac
    both = np.zeros((TOK, PREVPAD), np.float32)
    both[:, : PREV * PREV] = np.kron(up, up)
    return both


def dot(a, b):
    return jnp.dot(a, b, preferred_element_type=F32)


def dot_nt(a, b):
    return lax.dot_general(a, b, (((1,), (1,)), ((), ())), preferred_element_type=F32)


def pick(index, values):
    out = values[-1]
    for k in range(len(values) - 1):
        out = jnp.where(index == k, values[k], out)
    return out


def body(
    tok_h, quant_h, canvas_h, lift_h, loc_h, fac_h, sharp_s, qkv_h, wo_h, up_h, wd_h,
    kc_h, vc_h, fin_h, voc_h, kron_h,
    logits_h, canvas_o,
    tok, quant, canv, lift, loc, fac, woin, wdin, kc, vc, fin, voc, kron,
    wq, wo, wu, wd,
    emb, cout, st, nb1, nb2, nb3, qn, kn, vn, knc, att, attr, hid, pbuf, precv, lout,
    load_sem, own_sem, out_sem, cout_sem,
    us, ur, wos, wor, ats, atr, g2s, g2r, rss, rsr, g3s, g3r,
):
    me = lax.axis_index("tensor")
    dp = lax.axis_index("dp")
    mz = dp // 8
    my = lax.rem(dp // 2, 4)
    mc = lax.rem(dp, 2)
    right = lax.rem(me + 1, NX)
    left = lax.rem(me + 3, NX)
    opp = lax.rem(me + 2, NX)
    yp, ym, yo = lax.rem(my + 1, 4), lax.rem(my + 3, 4), lax.rem(my + 2, 4)
    zp, zm, zo = lax.rem(mz + 1, 4), lax.rem(mz + 3, 4), lax.rem(mz + 2, 4)

    def dpi(z, y, c):
        return {"dp": (z * 4 + y) * 2 + c}

    def rc(src, dst, s, r, dev):
        return pltpu.make_async_remote_copy(
            src_ref=src, dst_ref=dst, send_sem=s, recv_sem=r, device_id=dev, device_id_type=MESH
        )

    loads = [
        (tok_h, tok), (quant_h, quant), (canvas_h, canv), (lift_h, lift), (loc_h, loc),
        (fac_h, fac), (wo_h, woin), (wd_h, wdin), (kc_h, kc), (vc_h, vc), (fin_h, fin),
        (voc_h, voc), (kron_h, kron),
    ]

    def load(k):
        return pltpu.make_async_copy(loads[k][0], loads[k][1], load_sem.at[k])

    own_q = pltpu.make_async_copy(qkv_h, wq.at[mz, my, mc], own_sem.at[0])
    own_u = pltpu.make_async_copy(up_h, wu.at[mz, my, mc], own_sem.at[1])
    own_q.start()
    for k in (6, 7, 0, 1, 12, 2, 3, 4, 5):
        load(k).start()
    own_u.start()
    for k in (8, 9, 10, 11):
        load(k).start()

    barrier = pltpu.get_barrier_semaphore()
    peers = [{"tensor": right}, {"tensor": left}, {"tensor": opp}]
    peers += [dpi(mz, yp, mc), dpi(mz, ym, mc), dpi(zp, my, mc), dpi(zm, my, mc), dpi(mz, my, 1 - mc)]
    for dev in peers:
        pl.semaphore_signal(barrier, inc=1, device_id=dev, device_id_type=MESH)
    pl.semaphore_wait(barrier, len(peers))

    weights = (wq, wo, wu, wd)

    def unit_copies(r, v):
        w = weights[r]
        c0, c1, ch = SPLITS[r][v]
        u = 2 * r + v
        a, ap, am, ao = (my, yp, ym, yo) if v == 0 else (mz, zp, zm, zo)
        b, bp, bm, bo = (mz, zp, zm, zo) if v == 0 else (my, yp, ym, yo)

        def at(ai, bi, lo, hi):
            cols = pl.ds(lo, hi - lo)
            return w.at[bi, ai, mc, :, cols] if v == 0 else w.at[ai, bi, mc, :, cols]

        def dev(ai, bi):
            return dpi(bi, ai, mc) if v == 0 else dpi(ai, bi, mc)

        def copy(k, src, to):
            return rc(src, src, us.at[u, k], ur.at[u, k], to)

        send = [
            lambda: copy(0, at(a, b, c0, c1), dev(ap, b)),
            lambda: copy(1, at(a, b, c0, c1), dev(am, b)),
            lambda: copy(2, at(am, b, c0, ch), dev(ap, b)),
            lambda: copy(3, at(ap, b, ch, c1), dev(am, b)),
            lambda: copy(4, at(slice(None), b, c0, c1), dev(a, bp)),
            lambda: copy(5, at(slice(None), b, c0, c1), dev(a, bm)),
            lambda: copy(6, at(pl.ds(0, 2), bm, c0, c1), dev(a, bp)),
            lambda: copy(7, at(pl.ds(2, 2), bp, c0, c1), dev(a, bm)),
            lambda: copy(8, w.at[:, :, mc, :, pl.ds(c0, c1 - c0)], dpi(mz, my, 1 - mc)),
        ]
        recv = [
            lambda: copy(0, at(am, b, c0, c1), dev(ap, b)),
            lambda: copy(1, at(ap, b, c0, c1), dev(am, b)),
            lambda: copy(2, at(ao, b, c0, ch), dev(ap, b)),
            lambda: copy(3, at(ao, b, ch, c1), dev(am, b)),
            lambda: copy(4, at(slice(None), bm, c0, c1), dev(a, bp)),
            lambda: copy(5, at(slice(None), bp, c0, c1), dev(a, bm)),
            lambda: copy(6, at(pl.ds(0, 2), bo, c0, c1), dev(a, bp)),
            lambda: copy(7, at(pl.ds(2, 2), bo, c0, c1), dev(a, bm)),
            lambda: copy(8, w.at[:, :, 1 - mc, :, pl.ds(c0, c1 - c0)], dpi(mz, my, 1 - mc)),
        ]
        return send, recv

    def step(r, k):
        for i in (0, 1):
            for v in (0, 1):
                send, recv = unit_copies(r, v)
                if k == 1:
                    send[i]().start()
                elif k in (2, 4):
                    recv[2 * k - 4 + i]().wait_recv()
                    send[2 * k - 2 + i]().start()
                elif k in (3, 5):
                    if i == 0:
                        recv[2 * k - 4]().wait_recv()
                        recv[2 * k - 3]().wait_recv()
                        if k == 5:
                            send[8]().start()
                    if k == 3:
                        send[4 + i]().start()
                elif k == 6 and i == 0:
                    recv[8]().wait_recv()

    own_q.wait()
    step(0, 1)

    load(6).wait()
    load(7).wait()
    eye = (
        lax.broadcasted_iota(jnp.int32, (SH, SH), 0) == lax.broadcasted_iota(jnp.int32, (SH, SH), 1)
    ).astype(BF)
    mycols = pl.ds(pl.multiple_of(me * LW, 128), LW)
    wo[mz, my, mc, :, mycols] = dot_nt(eye, woin[...]).astype(BF)
    for n in range(3):
        wd[mz, my, mc, :, n * 512 : (n + 1) * 512] = dot_nt(
            eye, wdin[n * 512 : (n + 1) * 512, :]
        ).astype(BF)

    def wo_copy(k, owner, to):
        part = wo.at[mz, my, mc, :, pl.ds(pl.multiple_of(owner * LW, 128), LW)]
        return rc(part, part, wos.at[k], wor.at[k], {"tensor": to})

    wo_sends = [wo_copy(0, me, right), wo_copy(1, me, left), wo_copy(2, me, opp)]
    wo_recvs = [wo_copy(0, left, right), wo_copy(1, right, left), wo_copy(2, opp, opp)]
    for c in wo_sends:
        c.start()

    load(0).wait()
    load(1).wait()
    emb[...] = jnp.zeros_like(emb)

    def embed(n, carry):
        base = pl.multiple_of(n * 512, 512)
        ids = lax.broadcasted_iota(jnp.int32, (IMGS * PREVPAD, 512), 1) + base
        onehot = jnp.where(tok[...] == ids, 1.0, 0.0).astype(BF)
        emb[...] += dot(onehot, quant[pl.ds(base, 512), :].astype(BF))
        return carry

    lax.fori_loop(0, 4, embed, 0)
    step(0, 2)
    lax.fori_loop(4, 8, embed, 0)

    def modulated(rows_value, scale, shift):
        center = rows_value - jnp.mean(rows_value, axis=-1, keepdims=True)
        variance = jnp.mean(center * center, axis=-1, keepdims=True)
        return (center * lax.rsqrt(variance + FLOOR) * (1.0 + scale) + shift).astype(BF)

    for k in (12, 2, 3, 4, 5):
        load(k).wait()

    ORDER = (2, 1, 3, 0)

    def first_norm(jj, carry):
        j = lax.rem(me + pick(jj, ORDER), NX)
        rows = emb[pl.ds(pl.multiple_of(j * PREVPAD, 16), PREVPAD), :]
        lifted = lax.dot_general(
            kron[...], rows, (((1,), (0,)), ((), ())),
            precision=lax.Precision.HIGHEST, preferred_element_type=F32,
        )
        can = canv[j] + lifted
        cout[j] = can
        canb = can.astype(BF)
        for n in range(3):
            cols = slice(n * 512, (n + 1) * 512)
            st[:, cols] = dot(canb, lift[:, cols].astype(BF)) + loc[:, cols]
        scale = fac[j, 2:3, :]
        shift = fac[j, 4:5, :]

        def rows_norm(m, c):
            r = pl.ds(pl.multiple_of(m * 64, 64), 64)
            nb1[j, r, :] = modulated(st[r, :], scale, shift)
            return c

        lax.fori_loop(0, 4, rows_norm, 0)

        @pl.when(jj == 0)
        def _():
            step(0, 3)
            for c in wo_recvs:
                c.wait_recv()
            step(1, 1)

        return carry

    lax.fori_loop(0, 3, first_norm, 0)
    step(0, 4)
    step(1, 2)
    lax.fori_loop(3, 4, first_norm, 0)
    out_canvas = pltpu.make_async_copy(cout, canvas_o, cout_sem.at[0])
    out_canvas.start()

    load(8).wait()
    load(9).wait()

    def to_head(lanes):
        return (
            (lanes >= HDIM).astype(jnp.int32)
            + (lanes >= 2 * HDIM).astype(jnp.int32)
            + (lanes >= 3 * HDIM).astype(jnp.int32)
        )

    block_ones = jnp.where(to_head(lax.broadcasted_iota(jnp.int32, (LW, LW), 0))
        == to_head(lax.broadcasted_iota(jnp.int32, (LW, LW), 1)), 1.0, 0.0).astype(BF)
    lane_row = to_head(lax.broadcasted_iota(jnp.int32, (1, LW), 1))
    sharp = jnp.where(
        lane_row == 0,
        sharp_s[0, 0],
        jnp.where(lane_row == 1, sharp_s[0, 1], jnp.where(lane_row == 2, sharp_s[0, 2], sharp_s[0, 3])),
    )

    def unit(u):
        return u * lax.rsqrt(dot((u * u).astype(BF), block_ones) + 1.0)

    def cache_keys(j, carry):
        knc[j] = unit(kc[j].astype(F32)).astype(BF)
        return carry

    lax.fori_loop(0, 2, cache_keys, 0)
    step(0, 5)
    step(1, 3)
    own_u.wait()
    step(2, 1)
    lax.fori_loop(2, 4, cache_keys, 0)
    step(0, 6)

    def att_copy(jj, owner, to):
        return rc(att.at[jj], attr.at[owner], ats.at[jj], atr.at[jj], {"tensor": to})

    def attend(jj, carry):
        off = pick(jj, ORDER)
        j = lax.rem(me + off, NX)
        x = nb1[j]
        q = dot(x, wq[:, :, :, :, 0:LW].reshape(D, LW))
        qn[...] = (unit(q) * sharp).astype(BF)
        k = dot(x, wq[:, :, :, :, LW : 2 * LW].reshape(D, LW))
        kn[...] = unit(k).astype(BF)
        vn[...] = dot(x, wq[:, :, :, :, 2 * LW : 3 * LW].reshape(D, LW)).astype(BF)
        for h in range(HEADS_L):
            w0, w1 = WINDOWS[h]
            lanes = lax.broadcasted_iota(jnp.int32, (TOK, w1 - w0), 1) + w0
            mine = (lanes >= h * HDIM) & (lanes < (h + 1) * HDIM)
            qh = jnp.where(mine, qn[:, w0:w1], jnp.zeros((), BF))
            sc = dot_nt(qh, knc[j, :, w0:w1])
            sn = dot_nt(qh, kn[:, w0:w1])
            top = jnp.maximum(
                jnp.max(sc, axis=-1, keepdims=True), jnp.max(sn, axis=-1, keepdims=True)
            )
            pc = jnp.exp(sc - top)
            pn = jnp.exp(sn - top)
            total = jnp.sum(pc, axis=-1, keepdims=True) + jnp.sum(pn, axis=-1, keepdims=True)
            o = dot(pc.astype(BF), vc[j, :, w0:w1]) + dot(pn.astype(BF), vn[:, w0:w1])
            o = (o * (1.0 / total)).astype(BF)
            if h == 0:
                att[jj, :, w0:w1] = o
            else:
                att[jj, :, w0:w1] = jnp.where(mine, o, att[jj, :, w0:w1])

        @pl.when(jj == 0)
        def _():
            step(2, 2)
            step(1, 4)

        @pl.when(jj == 1)
        def _():
            step(2, 3)
            step(1, 5)
            step(3, 1)

        @pl.when(jj == 2)
        def _():
            step(3, 2)
            step(2, 4)

        @pl.when(jj < 3)
        def _():
            att_copy(jj, me, j).start()

        return carry

    att[...] = jnp.zeros_like(att)
    lax.fori_loop(0, 4, attend, 0)
    attr[me] = att[3]
    step(3, 3)
    step(2, 5)
    step(1, 6)
    for jj in range(3):
        att_copy(jj, lax.rem(me + 4 - ORDER[jj], NX), opp).wait_recv()

    def mix(z, carry):
        cols = pl.ds(pl.multiple_of(z * LW, 128), LW)
        mixed = jnp.zeros((TOK, LW), F32)
        for g in range(NX):
            w = wo[z, :, :, :, g * LW : (g + 1) * LW].reshape(LW, LW)
            mixed = mixed + dot_nt(attr[g], w).astype(BF).astype(F32)
        st[:, cols] = st[:, cols] + fac[me, 0:1, cols] * mixed
        return carry

    lax.fori_loop(0, 4, mix, 0)

    scale2 = fac[me, 3:4, :]
    shift2 = fac[me, 5:6, :]

    def second_norm(m, c):
        r = pl.ds(pl.multiple_of(m * 64, 64), 64)
        nb2[me, r, :] = modulated(st[r, :], scale2, shift2)
        return c

    lax.fori_loop(0, 4, second_norm, 0)

    H = (pl.ds(0, HALF), pl.ds(HALF, HALF))

    def gather_copies(nb, ss, rs):
        def c(k, img, half, to):
            ref = nb.at[img, H[half], :]
            return rc(ref, ref, ss.at[k], rs.at[k], {"tensor": to})

        send = [
            c(0, me, 0, right), c(1, me, 1, left), c(2, me, 1, right), c(3, me, 0, left),
            c(4, left, 0, right), c(5, right, 1, left),
        ]
        recv = [
            c(0, left, 0, right), c(1, right, 1, left), c(2, left, 1, right), c(3, right, 0, left),
            c(4, opp, 0, right), c(5, opp, 1, left),
        ]
        return send, recv

    def gather_steps(s, send, recv):
        @pl.when(s == 1)
        def _():
            recv[0].wait_recv()
            send[4].start()
            recv[1].wait_recv()
            send[5].start()

        @pl.when(s == 2)
        def _():
            recv[2].wait_recv()
            recv[3].wait_recv()

        @pl.when(s == 3)
        def _():
            recv[4].wait_recv()
            recv[5].wait_recv()

    def blocks(s):
        ia = lax.rem(me + pick(s, (0, 3, 3, 2)), NX)
        ib = lax.rem(me + pick(s, (0, 1, 1, 2)), NX)
        ha = pick(s, (0, 0, 1, 0))
        hb = pick(s, (1, 1, 0, 1))
        ra = pl.ds(pl.multiple_of(ha * HALF, HALF), HALF)
        rb = pl.ds(pl.multiple_of(hb * HALF, HALF), HALF)
        return ia, ra, ib, rb

    send2, recv2 = gather_copies(nb2, g2s, g2r)
    for k in range(4):
        send2[k].start()
    step(3, 4)
    step(2, 6)

    def part_copy(s, k, img, src_img, dst_rows):
        i = (s - 1) * 2 + k
        return rc(
            pbuf.at[s, H[k], :], precv.at[src_img, dst_rows, :], rss.at[i], rsr.at[i], {"tensor": img}
        )

    def feed_forward(s, carry):
        gather_steps(s, send2, recv2)
        ia, ra, ib, rb = blocks(s)

        def widen(n, c):
            cols = pl.ds(pl.multiple_of(n * LW, 128), LW)
            x = jnp.concatenate([nb2[ia, ra, :], nb2[ib, rb, :]], axis=0)
            u = dot(x, wu[:, :, :, :, cols].reshape(D, LW))
            act = 0.5 * u * (1.0 + jnp.tanh(0.7978845608028654 * (u + 0.044715 * (u * u * u))))
            hid[:, cols] = act.astype(BF)
            return c

        lax.fori_loop(0, 4, widen, 0)

        @pl.when(s == 0)
        def _():
            step(3, 5)
            step(3, 6)

        def narrow(z, c):
            cols = pl.ds(pl.multiple_of(z * LW, 128), LW)
            pbuf[s, :, cols] = dot_nt(hid[...], wd[z].reshape(LW, D)).astype(BF)
            return c

        lax.fori_loop(0, 4, narrow, 0)

        @pl.when(s >= 1)
        def _():
            part_copy(s, 0, ia, me, ra).start()
            part_copy(s, 1, ib, me, rb).start()

        return carry

    lax.fori_loop(0, 4, feed_forward, 0)

    part_recvs = [
        (1, 0, right, 0), (1, 1, left, 1), (2, 0, right, 1), (2, 1, left, 0), (3, 0, opp, 0), (3, 1, opp, 1),
    ]
    for s, k, src, half in part_recvs:
        part_copy(s, k, src, src, H[half]).wait_recv()
    load(10).wait()
    load(11).wait()

    gamma2 = fac[me, 1:2, :]
    scale3 = fin[me, 0:1, :]
    shift3 = fin[me, 1:2, :]

    def third_norm(m, c):
        r = pl.ds(pl.multiple_of(m * 64, 64), 64)
        mixed = pbuf[0, r, :].astype(F32) + precv[left, r, :].astype(F32)
        mixed = mixed + precv[right, r, :].astype(F32) + precv[opp, r, :].astype(F32)
        nb3[me, r, :] = modulated(st[r, :] + gamma2 * mixed, scale3, shift3)
        return c

    lax.fori_loop(0, 4, third_norm, 0)

    send3, recv3 = gather_copies(nb3, g3s, g3r)
    for k in range(4):
        send3[k].start()

    def out_copy(s, k, img, rows):
        return pltpu.make_async_copy(
            lout.at[s, H[k], :], logits_h.at[img, rows, :], out_sem.at[2 * s + k]
        )

    def head(s, carry):
        gather_steps(s, send3, recv3)
        ia, ra, ib, rb = blocks(s)

        def tile(n, c):
            cols = pl.ds(pl.multiple_of(n * 256, 256), 256)
            x = jnp.concatenate([nb3[ia, ra, :], nb3[ib, rb, :]], axis=0)
            lout[s, :, cols] = dot(x, voc[:, cols]).astype(BF)
            return c

        lax.fori_loop(0, 4, tile, 0)
        out_copy(s, 0, ia, ra).start()
        out_copy(s, 1, ib, rb).start()
        return carry

    lax.fori_loop(0, 4, head, 0)

    for r in range(4):
        for v in (0, 1):
            send, _ = unit_copies(r, v)
            for k in range(9):
                send[k]().wait_send()
    for c in wo_sends:
        c.wait_send()
    for jj in range(3):
        att_copy(jj, me, opp).wait_send()
    for k in range(6):
        send2[k].wait_send()
        send3[k].wait_send()
    for s, k, src, half in part_recvs:
        part_copy(s, k, src, src, H[half]).wait_send()
    out_canvas.wait()

    def out_done(s, carry):
        ia, ra, ib, rb = blocks(s)
        out_copy(s, 0, ia, ra).wait()
        out_copy(s, 1, ib, rb).wait()
        return carry

    lax.fori_loop(0, 4, out_done, 0)


def local(
    sampled_earlier_tokens,
    quantizer_vectors,
    summed_latent_canvas,
    latent_lift_matrix,
    location_tier_offset,
    adaptive_norm_factors,
    logit_sharpness,
    probe_match_content_matrix,
    mixing_projection_matrix,
    widening_projection_matrix,
    narrowing_projection_matrix,
    cached_lower_grid_lookups,
    cached_lower_grid_payloads,
    final_norm_factors,
    vocabulary_logit_matrix,
):
    tokens = jnp.pad(sampled_earlier_tokens, ((0, 0), (0, PREVPAD - PREV * PREV)), constant_values=-1)
    tokens = tokens.reshape(IMGS * PREVPAD, 1)
    operands = (
        tokens,
        quantizer_vectors,
        summed_latent_canvas,
        latent_lift_matrix,
        location_tier_offset,
        adaptive_norm_factors[0],
        logit_sharpness,
        probe_match_content_matrix[0].reshape(SH, 3 * LW),
        mixing_projection_matrix[0],
        widening_projection_matrix[0],
        narrowing_projection_matrix[0],
        cached_lower_grid_lookups[0],
        cached_lower_grid_payloads[0],
        final_norm_factors,
        vocabulary_logit_matrix,
        jnp.asarray(upsample_matrix()),
    )
    anyspace = pl.BlockSpec(memory_space=pl.ANY)
    specs = [anyspace] * len(operands)
    specs[6] = pl.BlockSpec(memory_space=pltpu.SMEM)
    vm = pltpu.VMEM
    dma = pltpu.SemaphoreType.DMA
    scratch = [
        vm((IMGS * PREVPAD, 1), jnp.int32),
        vm((VOCAB, CVAE), F32),
        vm((IMGS, TOK, CVAE), F32),
        vm((CVAE, D), F32),
        vm((TOK, D), F32),
        vm((IMGS, 6, D), F32),
        vm((LW, SH), BF),
        vm((D, SH), BF),
        vm((IMGS, CACHE, LW), BF),
        vm((IMGS, CACHE, LW), BF),
        vm((IMGS, 2, D), F32),
        vm((D, VL), BF),
        vm((TOK, PREVPAD), F32),
        vm((4, 4, 2, SH, 3 * LW), BF),
        vm((4, 4, 2, SH, D), BF),
        vm((4, 4, 2, SH, D), BF),
        vm((4, 4, 2, SH, D), BF),
        vm((IMGS * PREVPAD, CVAE), F32),
        vm((IMGS, TOK, CVAE), F32),
        vm((TOK, D), F32),
        vm((IMGS, TOK, D), BF),
        vm((IMGS, TOK, D), BF),
        vm((IMGS, TOK, D), BF),
        vm((TOK, LW), BF),
        vm((TOK, LW), BF),
        vm((TOK, LW), BF),
        vm((IMGS, CACHE, LW), BF),
        vm((NX, TOK, LW), BF),
        vm((NX, TOK, LW), BF),
        vm((TOK, D), BF),
        vm((NX, TOK, D), BF),
        vm((NX, TOK, D), BF),
        vm((NX, TOK, VL), BF),
        dma((13,)), dma((2,)), dma((8,)), dma((1,)),
        dma((8, 9)), dma((8, 9)), dma((3,)), dma((3,)), dma((3,)), dma((3,)),
        dma((6,)), dma((6,)), dma((6,)), dma((6,)), dma((6,)), dma((6,)),
    ]
    return pl.pallas_call(
        body,
        out_shape=(
            jax.ShapeDtypeStruct((IMGS, TOK, VL), BF),
            jax.ShapeDtypeStruct((IMGS, TOK, CVAE), F32),
        ),
        in_specs=specs,
        out_specs=(anyspace, anyspace),
        scratch_shapes=scratch,
        compiler_params=pltpu.CompilerParams(
            collective_id=0, has_side_effects=True, vmem_limit_bytes=67_000_000
        ),
    )(*operands)


def solution(mesh):
    placed = (
        P("dp", None),
        P(),
        P("dp", None, None),
        P(),
        P(),
        P(None, "dp", None, None),
        P(None, "tensor"),
        P(None, "dp", None, "tensor"),
        P(None, "tensor", "dp"),
        P(None, "dp", "tensor"),
        P(None, "tensor", "dp"),
        P(None, "dp", None, "tensor"),
        P(None, "dp", None, "tensor"),
        P("dp", None, None),
        P(None, "tensor"),
    )
    return jax.shard_map(
        local,
        mesh=mesh,
        in_specs=placed,
        out_specs=(P("dp", None, "tensor"), P("dp", None, None)),
        check_vma=False,
    )
```

profile of v0, /device:TPU:8, one launch (start us, length us, event | category | flops | bytes accessed | tf_op | source)
XLA Modules:
  0.0 169.3 jit_solution(889249882191666905)
XLA Ops:
  0.6 0.0 copy-start
  0.6 0.8 pad.4
  1.4 1.5 copy.27
  2.9 1.0 copy.26
  3.8 0.7 copy.33
  4.5 1.6 copy.35
  6.1 0.9 reshape.8.tok_h
  7.1 1.8 %copy.28 = bf16[1,1536,48]{2,1,0:T(8,128)(2,1)} copy(bf16[1,1536,48]{1,2,0:T(8,128)(2,1)} %param.26) | data formatting | bytes 294912 | tf_op args[10]
  8.9 1.9 %copy.31.canvas_h = f32[4,256,32]{2,1,0:T(8,128)} copy(f32[4,256,32]{1,2,0:T(8,128)} %param.18) | data formatting | bytes 262144 | tf_op args[2]
  10.8 0.0 copy-done
  10.8 1.9 %copy.30.quant_h = f32[4096,32]{1,0:T(8,128)} copy(f32[4096,32]{0,1:T(8,128)S(1)} %copy-done) | data formatting | bytes 1048576 | tf_op args[1]
  12.7 151.6 %shard_map.167 = (bf16[4,256,1024]{2,1,0:T(8,128)(2,1)}, f32[4,256,32]{2,1,0:T(8,128)}) custom-call(s32[704,1]{1,0:T(8,128)} %reshape.8.tok_h, f32[4096,32]{1,0:T(8,128)} %copy.30.quant_h, f32[4,256,32]{2,1,0:T(8,128)} %copy.31.canvas_h, f32[32,1536]{1,0:T(8,128)} %lift_h.1, f32[256,1536]{1,0:T(8,128)} %loc_h.1, f32[4,6,1536]{2,1,0:T(8,128)} %bitcast.14, ...), custom_call_target="tpu_custom_call" | custom-call | tf_op jit(solution)/shard_map/pallas_call | solution.py:635
  164.3 1.9 %copy.32 = f32[4,256,32]{1,2,0:T(8,128)} copy(f32[4,256,32]{2,1,0:T(8,128)} %get-tuple-element.5) | data formatting | bytes 262144 | tf_op jit(solution)/shard_map/pallas_call | solution.py:635
  166.2 3.1 %copy.37 = bf16[4,256,1024]{2,1,0:T(8,128)(2,1)} copy(bf16[4,256,1024]{2,1,0:T(8,128)(2,1)} %get-tuple-element.8) | data formatting | bytes 4194304
Async XLA Ops:
  0.6 10.2 %copy-start = (f32[4096,32]{0,1:T(8,128)S(1)}, f32[4096,32]{0,1:T(8,128)}, u32[]{:S(2)}) copy-start(f32[4096,32]{0,1:T(8,128)} %param.17) | copy-start | bytes 1572868
where the time goes:
time: 170 us; the launch traced here: 169 us
  Pallas kernels  152 us (89%)
  local copies, waits for them, and re-layouts  17.1 us (10%)
    pallas_call x1, Pallas kernels, local(): pl.pallas_call(body, out_shape=(jax.ShapeDtypeStruct((IMGS, TOK, VL), BF)...  152 us
    unnamed x10, local copies, waits for them, and re-layouts  13.5 us

commit v1 on v0

--- a/solution.py
+++ b/solution.py
@@ -19,7 +19,7 @@
 CVAE = 32
 SIDE = 16
 PREV = 13
-PREVPAD = 176
+PREVTOK = 169
 CACHE = 424
 TOK = 256
 HALF = 128
@@ -46,9 +46,7 @@
     up = np.zeros((SIDE, PREV))
     up[a, low] += 1.0 - frac
     up[a, np.minimum(low + 1, PREV - 1)] += frac
-    both = np.zeros((TOK, PREVPAD), np.float32)
-    both[:, : PREV * PREV] = np.kron(up, up)
-    return both
+    return np.kron(up, up).T.astype(np.float32)
 
 
 def dot(a, b):
@@ -70,7 +68,7 @@
     tok_h, quant_h, canvas_h, lift_h, loc_h, fac_h, sharp_s, qkv_h, wo_h, up_h, wd_h,
     kc_h, vc_h, fin_h, voc_h, kron_h,
     logits_h, canvas_o,
-    tok, quant, canv, lift, loc, fac, woin, wdin, kc, vc, fin, voc, kron,
+    tok, quant, canv, lift, loc, fac, kc, vc, fin, voc, kron,
     wq, wo, wu, wd,
     emb, cout, st, nb1, nb2, nb3, qn, kn, vn, knc, att, attr, hid, pbuf, precv, lout,
     load_sem, own_sem, out_sem, cout_sem,
@@ -95,18 +93,25 @@
             src_ref=src, dst_ref=dst, send_sem=s, recv_sem=r, device_id=dev, device_id_type=MESH
         )
 
+    mycols = pl.ds(pl.multiple_of(me * LW, 128), LW)
     loads = [
         (tok_h, tok), (quant_h, quant), (canvas_h, canv), (lift_h, lift), (loc_h, loc),
-        (fac_h, fac), (wo_h, woin), (wd_h, wdin), (kc_h, kc), (vc_h, vc), (fin_h, fin),
-        (voc_h, voc), (kron_h, kron),
+        (fac_h, fac), (wo_h, wo.at[mz, my, mc, :, mycols]), (wd_h, wd.at[mz, my, mc]),
+        (kc_h, kc), (vc_h, vc), (fin_h, fin), (voc_h, voc), (kron_h, kron),
     ]
 
     def load(k):
         return pltpu.make_async_copy(loads[k][0], loads[k][1], load_sem.at[k])
 
-    own_q = pltpu.make_async_copy(qkv_h, wq.at[mz, my, mc], own_sem.at[0])
-    own_u = pltpu.make_async_copy(up_h, wu.at[mz, my, mc], own_sem.at[1])
-    own_q.start()
+    own_q = [
+        pltpu.make_async_copy(
+            qkv_h.at[k], wq.at[mz, my, mc, :, pl.ds(k * LW, LW)], own_sem.at[1 + k]
+        )
+        for k in range(3)
+    ]
+    own_u = pltpu.make_async_copy(up_h, wu.at[mz, my, mc], own_sem.at[0])
+    for c in own_q:
+        c.start()
     for k in (6, 7, 0, 1, 12, 2, 3, 4, 5):
         load(k).start()
     own_u.start()
@@ -183,20 +188,12 @@
                 elif k == 6 and i == 0:
                     recv[8]().wait_recv()
 
-    own_q.wait()
+    for c in own_q:
+        c.wait()
     step(0, 1)
 
     load(6).wait()
     load(7).wait()
-    eye = (
-        lax.broadcasted_iota(jnp.int32, (SH, SH), 0) == lax.broadcasted_iota(jnp.int32, (SH, SH), 1)
-    ).astype(BF)
-    mycols = pl.ds(pl.multiple_of(me * LW, 128), LW)
-    wo[mz, my, mc, :, mycols] = dot_nt(eye, woin[...]).astype(BF)
-    for n in range(3):
-        wd[mz, my, mc, :, n * 512 : (n + 1) * 512] = dot_nt(
-            eye, wdin[n * 512 : (n + 1) * 512, :]
-        ).astype(BF)
 
     def wo_copy(k, owner, to):
         part = wo.at[mz, my, mc, :, pl.ds(pl.multiple_of(owner * LW, 128), LW)]
@@ -211,11 +208,17 @@
     load(1).wait()
     emb[...] = jnp.zeros_like(emb)
 
+    def high_low(v):
+        high = v.astype(BF)
+        return high, (v - high.astype(F32)).astype(BF)
+
     def embed(n, carry):
         base = pl.multiple_of(n * 512, 512)
-        ids = lax.broadcasted_iota(jnp.int32, (IMGS * PREVPAD, 512), 1) + base
-        onehot = jnp.where(tok[...] == ids, 1.0, 0.0).astype(BF)
-        emb[...] += dot(onehot, quant[pl.ds(base, 512), :].astype(BF))
+        table = jnp.concatenate(high_low(quant[:, pl.ds(base, 512)]), axis=0)
+        ids = lax.broadcasted_iota(jnp.int32, (512, PREVTOK), 0) + base
+        for j in range(IMGS):
+            onehot = jnp.where(tok[j : j + 1, :] == ids, 1.0, 0.0).astype(BF)
+            emb[j] += dot(table, onehot)
         return carry
 
     lax.fori_loop(0, 4, embed, 0)
@@ -234,19 +237,24 @@
 
     def first_norm(jj, carry):
         j = lax.rem(me + pick(jj, ORDER), NX)
-        rows = emb[pl.ds(pl.multiple_of(j * PREVPAD, 16), PREVPAD), :]
+        rows = emb[j, 0:CVAE, :] + emb[j, CVAE : 2 * CVAE, :]
         lifted = lax.dot_general(
-            kron[...], rows, (((1,), (0,)), ((), ())),
+            rows, kron[...], (((1,), (0,)), ((), ())),
             precision=lax.Precision.HIGHEST, preferred_element_type=F32,
         )
         can = canv[j] + lifted
         cout[j] = can
-        canb = can.astype(BF)
+        can_hi, can_lo = high_low(can)
+        can3 = jnp.concatenate([can_hi, can_lo, can_hi], axis=0)
         for n in range(3):
             cols = slice(n * 512, (n + 1) * 512)
-            st[:, cols] = dot(canb, lift[:, cols].astype(BF)) + loc[:, cols]
-        scale = fac[j, 2:3, :]
-        shift = fac[j, 4:5, :]
+            lift_hi, lift_lo = high_low(lift[:, cols])
+            lift3 = jnp.concatenate([lift_hi, lift_hi, lift_lo], axis=0)
+            st[:, cols] = loc[:, cols] + lax.dot_general(
+                can3, lift3, (((0,), (0,)), ((), ())), preferred_element_type=F32
+            )
+        scale = fac[2, pl.ds(j, 1), :]
+        shift = fac[4, pl.ds(j, 1), :]
 
         def rows_norm(m, c):
             r = pl.ds(pl.multiple_of(m * 64, 64), 64)
@@ -374,13 +382,13 @@
         for g in range(NX):
             w = wo[z, :, :, :, g * LW : (g + 1) * LW].reshape(LW, LW)
             mixed = mixed + dot_nt(attr[g], w).astype(BF).astype(F32)
-        st[:, cols] = st[:, cols] + fac[me, 0:1, cols] * mixed
+        st[:, cols] = st[:, cols] + fac[0, pl.ds(me, 1), cols] * mixed
         return carry
 
     lax.fori_loop(0, 4, mix, 0)
 
-    scale2 = fac[me, 3:4, :]
-    shift2 = fac[me, 5:6, :]
+    scale2 = fac[3, pl.ds(me, 1), :]
+    shift2 = fac[5, pl.ds(me, 1), :]
 
     def second_norm(m, c):
         r = pl.ds(pl.multiple_of(m * 64, 64), 64)
@@ -488,7 +496,7 @@
     load(10).wait()
     load(11).wait()
 
-    gamma2 = fac[me, 1:2, :]
+    gamma2 = fac[1, pl.ds(me, 1), :]
     scale3 = fin[me, 0:1, :]
     shift3 = fin[me, 1:2, :]
 
@@ -569,20 +577,18 @@
     final_norm_factors,
     vocabulary_logit_matrix,
 ):
-    tokens = jnp.pad(sampled_earlier_tokens, ((0, 0), (0, PREVPAD - PREV * PREV)), constant_values=-1)
-    tokens = tokens.reshape(IMGS * PREVPAD, 1)
     operands = (
-        tokens,
-        quantizer_vectors,
-        summed_latent_canvas,
+        sampled_earlier_tokens,
+        quantizer_vectors.T,
+        jnp.swapaxes(summed_latent_canvas, 1, 2),
         latent_lift_matrix,
         location_tier_offset,
-        adaptive_norm_factors[0],
+        jnp.swapaxes(adaptive_norm_factors[0], 0, 1),
         logit_sharpness,
-        probe_match_content_matrix[0].reshape(SH, 3 * LW),
-        mixing_projection_matrix[0],
+        jnp.swapaxes(probe_match_content_matrix[0], 0, 1),
+        mixing_projection_matrix[0].T,
         widening_projection_matrix[0],
-        narrowing_projection_matrix[0],
+        narrowing_projection_matrix[0].T,
         cached_lower_grid_lookups[0],
         cached_lower_grid_payloads[0],
         final_norm_factors,
@@ -595,25 +601,23 @@
     vm = pltpu.VMEM
     dma = pltpu.SemaphoreType.DMA
     scratch = [
-        vm((IMGS * PREVPAD, 1), jnp.int32),
-        vm((VOCAB, CVAE), F32),
-        vm((IMGS, TOK, CVAE), F32),
+        vm((IMGS, PREVTOK), jnp.int32),
+        vm((CVAE, VOCAB), F32),
+        vm((IMGS, CVAE, TOK), F32),
         vm((CVAE, D), F32),
         vm((TOK, D), F32),
-        vm((IMGS, 6, D), F32),
-        vm((LW, SH), BF),
-        vm((D, SH), BF),
+        vm((6, IMGS, D), F32),
         vm((IMGS, CACHE, LW), BF),
         vm((IMGS, CACHE, LW), BF),
         vm((IMGS, 2, D), F32),
         vm((D, VL), BF),
-        vm((TOK, PREVPAD), F32),
+        vm((PREVTOK, TOK), F32),
         vm((4, 4, 2, SH, 3 * LW), BF),
         vm((4, 4, 2, SH, D), BF),
         vm((4, 4, 2, SH, D), BF),
         vm((4, 4, 2, SH, D), BF),
-        vm((IMGS * PREVPAD, CVAE), F32),
-        vm((IMGS, TOK, CVAE), F32),
+        vm((IMGS, 2 * CVAE, PREVTOK), F32),
+        vm((IMGS, CVAE, TOK), F32),
         vm((TOK, D), F32),
         vm((IMGS, TOK, D), BF),
         vm((IMGS, TOK, D), BF),
@@ -628,15 +632,15 @@
         vm((NX, TOK, D), BF),
         vm((NX, TOK, D), BF),
         vm((NX, TOK, VL), BF),
-        dma((13,)), dma((2,)), dma((8,)), dma((1,)),
+        dma((13,)), dma((4,)), dma((8,)), dma((1,)),
         dma((8, 9)), dma((8, 9)), dma((3,)), dma((3,)), dma((3,)), dma((3,)),
         dma((6,)), dma((6,)), dma((6,)), dma((6,)), dma((6,)), dma((6,)),
     ]
-    return pl.pallas_call(
+    logits, canvas = pl.pallas_call(
         body,
         out_shape=(
             jax.ShapeDtypeStruct((IMGS, TOK, VL), BF),
-            jax.ShapeDtypeStruct((IMGS, TOK, CVAE), F32),
+            jax.ShapeDtypeStruct((IMGS, CVAE, TOK), F32),
         ),
         in_specs=specs,
         out_specs=(anyspace, anyspace),
@@ -645,6 +649,7 @@
             collective_id=0, has_side_effects=True, vmem_limit_bytes=67_000_000
         ),
     )(*operands)
+    return logits, jnp.swapaxes(canvas, 1, 2)
 
 
 def solution(mesh):

time: 170 us -> 158 us (0.929)
  local copies, waits for them, and re-layouts: 17.1 us -> 3.77 us
    unnamed x10 -> x4, local copies, waits for them, and re-layouts: 13.5 us -> 3.77 us
    pallas_call x1 -> x0, local copies, waits for them, and re-layouts: 1.87 us -> none  [local(): pl.pallas_call(body, out_shape=(jax.ShapeDtypeStruct((IMGS, TOK, VL), BF)...]
where the time goes in v1:
time: 158 us; the launch traced here: 157 us
  Pallas kernels  153 us (97%)
  local copies, waits for them, and re-layouts  3.77 us (2%)
    pallas_call x1, Pallas kernels, local(): pl.pallas_call(body, out_shape=(jax.ShapeDtypeStruct((IMGS, TOK, VL), BF)...  153 us
    unnamed x4, local copies, waits for them, and re-layouts  3.77 us

profile of v1, /device:TPU:8, one launch (start us, length us, event | category | flops | bytes accessed | tf_op | source)
XLA Modules:
  0.0 157.5 jit_solution(14530156466886976126)
XLA Ops:
  0.6 153.0 %shard_map.167 = (bf16[4,256,1024]{2,1,0:T(8,128)(2,1)}, f32[4,32,256]{2,1,0:T(8,128)}) custom-call(s32[4,169]{1,0:T(4,128)} %tok_h.1, f32[32,4096]{1,0:T(8,128)} %bitcast.20, f32[4,32,256]{2,1,0:T(8,128)} %bitcast.24, f32[32,1536]{1,0:T(8,128)} %lift_h.1, f32[256,1536]{1,0:T(8,128)} %loc_h.1, f32[6,4,1536]{2,1,0:T(4,128)} %bitcast.21, f32[1,4]{1,0:T(1,128)} %sharp_s.1, ...), custom_call_target="tpu_custom_call" | custom-call | tf_op jit(solution)/shard_map/pallas_call | solution.py:639
  153.7 0.0 copy-start
  153.7 3.1 %copy.20 = bf16[4,256,1024]{2,1,0:T(8,128)(2,1)} copy(bf16[4,256,1024]{2,1,0:T(8,128)(2,1)} %get-tuple-element.8) | data formatting | bytes 4194304
  156.8 0.0 copy-done
  156.8 0.7 copy.21
Async XLA Ops:
  153.7 3.1 %copy-start = (f32[4,32,256]{2,1,0:T(8,128)S(1)}, f32[4,32,256]{2,1,0:T(8,128)}, u32[]{:S(2)}) copy-start(f32[4,32,256]{2,1,0:T(8,128)} %get-tuple-element.5) | copy-start | bytes 393220

commit v2 on v1

--- a/solution.py
+++ b/solution.py
@@ -23,6 +23,7 @@
 CACHE = 424
 TOK = 256
 HALF = 128
+QUART = 64
 IMGS = 4
 SH = 48
 NX = 4
@@ -30,12 +31,8 @@
 
 WINDOWS = ((0, 128), (0, 256), (128, 384), (256, 384))
 
-SPLITS = (
-    ((0, 640, 384), (640, 1152, 896)),
-    ((0, 768, 384), (768, 1536, 1152)),
-    ((0, 768, 384), (768, 1536, 1152)),
-    ((0, 768, 384), (768, 1536, 1152)),
-)
+QKV_SPLIT = ((0, 640, 384), (640, 1152, 896))
+SPLIT = ((0, 768, 384), (768, 1536, 1152))
 
 
 def upsample_matrix():
@@ -70,9 +67,9 @@
     logits_h, canvas_o,
     tok, quant, canv, lift, loc, fac, kc, vc, fin, voc, kron,
     wq, wo, wu, wd,
-    emb, cout, st, nb1, nb2, nb3, qn, kn, vn, knc, att, attr, hid, pbuf, precv, lout,
+    emb, cout, st, nb1, nb2, nb3, qn, kn, vn, knc, att, attr, hid, pbuf, precv, pacc, lout,
     load_sem, own_sem, out_sem, cout_sem,
-    us, ur, wos, wor, ats, atr, g2s, g2r, rss, rsr, g3s, g3r,
+    qs, qr, us, ur, wos, wor, ats, atr, g2s, g2r, rss, rsr, g3s, g3r,
 ):
     me = lax.axis_index("tensor")
     dp = lax.axis_index("dp")
@@ -125,24 +122,79 @@
         pl.semaphore_signal(barrier, inc=1, device_id=dev, device_id_type=MESH)
     pl.semaphore_wait(barrier, len(peers))
 
-    weights = (wq, wo, wu, wd)
+    weights = (wo, wu, wd)
+
+    def ring(w, split, v, sends, recvs):
+        c0, c1, ch = split[v]
+        a, ap, am, ao = (my, yp, ym, yo) if v == 0 else (mz, zp, zm, zo)
+        b, bp, bm, bo = (mz, zp, zm, zo) if v == 0 else (my, yp, ym, yo)
+
+        def at(ai, bi, lo, hi, core=mc):
+            cols = pl.ds(lo, hi - lo)
+            return w.at[bi, ai, core, :, cols] if v == 0 else w.at[ai, bi, core, :, cols]
+
+        def dev(ai, bi):
+            return dpi(bi, ai, mc) if v == 0 else dpi(ai, bi, mc)
+
+        def copy(k, src, to):
+            return rc(src, src, sends.at[k], recvs.at[k], to)
+
+        return c0, c1, ch, (a, ap, am, ao), (b, bp, bm, bo), at, dev, copy
+
+    other = dpi(mz, my, 1 - mc)
+
+    def qkv_copies(v):
+        c0, c1, ch, (a, ap, am, ao), (b, bp, bm, bo), at, dev, copy = ring(
+            wq, QKV_SPLIT, v, qs.at[v], qr.at[v]
+        )
+        every = slice(None)
+        row = (a, am, ap, ao)
+        send = [
+            (at(a, b, c0, c1), dev(ap, b)),
+            (at(a, b, c0, c1), dev(am, b)),
+            (at(am, b, c0, ch), dev(ap, b)),
+            (at(ap, b, ch, c1), dev(am, b)),
+        ]
+        recv = [at(am, b, c0, c1), at(ap, b, c0, c1), at(ao, b, c0, ch), at(ao, b, ch, c1)]
+        send += [(at(ai, b, c0, c1), dev(a, bp)) for ai in row]
+        recv += [at(ai, bm, c0, c1) for ai in row]
+        send += [(at(ai, b, c0, c1), dev(a, bm)) for ai in row]
+        recv += [at(ai, bp, c0, c1) for ai in row]
+        send += [(at(ai, bm, c0, c1), dev(a, bp)) for ai in row[:2]]
+        send += [(at(ai, bp, c0, c1), dev(a, bm)) for ai in row[2:]]
+        recv += [at(ai, bo, c0, c1) for ai in row]
+        send += [(at(every, bi, c0, c1), other) for bi in (b, bm, bp, bo)]
+        recv += [at(every, bi, c0, c1, 1 - mc) for bi in (b, bm, bp, bo)]
+        return (
+            [lambda k=k, x=x: copy(k, *x) for k, x in enumerate(send)],
+            [lambda k=k, x=x: copy(k, x, other) for k, x in enumerate(recv)],
+        )
+
+    QKV_STAGES = (
+        (((), (0, 1, 4, 8)),),
+        (((0,), (2, 5, 9)), ((1,), (3, 6, 10))),
+        (((2, 3), (7, 11, 16)),),
+        (((4,), (12,)), ((5,), (13,)), ((10,), (14,))),
+        (((11,), (15,)), ((6, 7), (17,)), ((8, 9), (18,))),
+        (((12, 13, 14, 15), (19,)),),
+        (((16, 17, 18, 19), ()),),
+    )
+
+    def qkv_stage(k):
+        for waits, starts in QKV_STAGES[k]:
+            for v in (0, 1):
+                send, recv = qkv_copies(v)
+                for i in waits:
+                    recv[i]().wait_recv()
+                for i in starts:
+                    send[i]().start()
 
     def unit_copies(r, v):
         w = weights[r]
-        c0, c1, ch = SPLITS[r][v]
         u = 2 * r + v
-        a, ap, am, ao = (my, yp, ym, yo) if v == 0 else (mz, zp, zm, zo)
-        b, bp, bm, bo = (mz, zp, zm, zo) if v == 0 else (my, yp, ym, yo)
-
-        def at(ai, bi, lo, hi):
-            cols = pl.ds(lo, hi - lo)
-            return w.at[bi, ai, mc, :, cols] if v == 0 else w.at[ai, bi, mc, :, cols]
-
-        def dev(ai, bi):
-            return dpi(bi, ai, mc) if v == 0 else dpi(ai, bi, mc)
-
-        def copy(k, src, to):
-            return rc(src, src, us.at[u, k], ur.at[u, k], to)
+        c0, c1, ch, (a, ap, am, ao), (b, bp, bm, bo), at, dev, copy = ring(
+            w, SPLIT, v, us.at[u], ur.at[u]
+        )
 
         send = [
             lambda: copy(0, at(a, b, c0, c1), dev(ap, b)),
@@ -153,7 +205,7 @@
             lambda: copy(5, at(slice(None), b, c0, c1), dev(a, bm)),
             lambda: copy(6, at(pl.ds(0, 2), bm, c0, c1), dev(a, bp)),
             lambda: copy(7, at(pl.ds(2, 2), bp, c0, c1), dev(a, bm)),
-            lambda: copy(8, w.at[:, :, mc, :, pl.ds(c0, c1 - c0)], dpi(mz, my, 1 - mc)),
+            lambda: copy(8, w.at[:, :, mc, :, pl.ds(c0, c1 - c0)], other),
         ]
         recv = [
             lambda: copy(0, at(am, b, c0, c1), dev(ap, b)),
@@ -164,7 +216,7 @@
             lambda: copy(5, at(slice(None), bp, c0, c1), dev(a, bm)),
             lambda: copy(6, at(pl.ds(0, 2), bo, c0, c1), dev(a, bp)),
             lambda: copy(7, at(pl.ds(2, 2), bo, c0, c1), dev(a, bm)),
-            lambda: copy(8, w.at[:, :, 1 - mc, :, pl.ds(c0, c1 - c0)], dpi(mz, my, 1 - mc)),
+            lambda: copy(8, w.at[:, :, 1 - mc, :, pl.ds(c0, c1 - c0)], other),
         ]
         return send, recv
 
@@ -190,7 +242,7 @@
 
     for c in own_q:
         c.wait()
-    step(0, 1)
+    qkv_stage(0)
 
     load(6).wait()
     load(7).wait()
@@ -221,9 +273,13 @@
             emb[j] += dot(table, onehot)
         return carry
 
-    lax.fori_loop(0, 4, embed, 0)
-    step(0, 2)
-    lax.fori_loop(4, 8, embed, 0)
+    lax.fori_loop(0, 5, embed, 0)
+    qkv_stage(1)
+    own_u.wait()
+    step(1, 1)
+    lax.fori_loop(5, 8, embed, 0)
+    qkv_stage(2)
+    step(2, 1)
 
     def modulated(rows_value, scale, shift):
         center = rows_value - jnp.mean(rows_value, axis=-1, keepdims=True)
@@ -265,17 +321,29 @@
 
         @pl.when(jj == 0)
         def _():
-            step(0, 3)
+            qkv_stage(3)
             for c in wo_recvs:
                 c.wait_recv()
-            step(1, 1)
+            step(0, 1)
+
+        @pl.when(jj == 1)
+        def _():
+            qkv_stage(4)
+            step(0, 2)
+
+        @pl.when(jj == 2)
+        def _():
+            step(1, 2)
+
+        @pl.when(jj == 3)
+        def _():
+            qkv_stage(5)
+            step(0, 3)
+            step(2, 2)
 
         return carry
 
-    lax.fori_loop(0, 3, first_norm, 0)
-    step(0, 4)
-    step(1, 2)
-    lax.fori_loop(3, 4, first_norm, 0)
+    lax.fori_loop(0, 4, first_norm, 0)
     out_canvas = pltpu.make_async_copy(cout, canvas_o, cout_sem.at[0])
     out_canvas.start()
 
@@ -305,13 +373,9 @@
         knc[j] = unit(kc[j].astype(F32)).astype(BF)
         return carry
 
-    lax.fori_loop(0, 2, cache_keys, 0)
-    step(0, 5)
+    lax.fori_loop(0, 4, cache_keys, 0)
+    qkv_stage(6)
     step(1, 3)
-    own_u.wait()
-    step(2, 1)
-    lax.fori_loop(2, 4, cache_keys, 0)
-    step(0, 6)
 
     def att_copy(jj, owner, to):
         return rc(att.at[jj], attr.at[owner], ats.at[jj], atr.at[jj], {"tensor": to})
@@ -347,19 +411,15 @@
 
         @pl.when(jj == 0)
         def _():
-            step(2, 2)
+            step(0, 4)
+
+        @pl.when(jj == 1)
+        def _():
+            step(2, 3)
+
+        @pl.when(jj == 2)
+        def _():
             step(1, 4)
-
-        @pl.when(jj == 1)
-        def _():
-            step(2, 3)
-            step(1, 5)
-            step(3, 1)
-
-        @pl.when(jj == 2)
-        def _():
-            step(3, 2)
-            step(2, 4)
 
         @pl.when(jj < 3)
         def _():
@@ -370,11 +430,11 @@
     att[...] = jnp.zeros_like(att)
     lax.fori_loop(0, 4, attend, 0)
     attr[me] = att[3]
-    step(3, 3)
-    step(2, 5)
-    step(1, 6)
+    step(0, 5)
     for jj in range(3):
         att_copy(jj, lax.rem(me + 4 - ORDER[jj], NX), opp).wait_recv()
+    step(2, 4)
+    step(0, 6)
 
     def mix(z, carry):
         cols = pl.ds(pl.multiple_of(z * LW, 128), LW)
@@ -395,66 +455,78 @@
         nb2[me, r, :] = modulated(st[r, :], scale2, shift2)
         return c
 
-    lax.fori_loop(0, 4, second_norm, 0)
-
-    H = (pl.ds(0, HALF), pl.ds(HALF, HALF))
+    def rows_at(first, count):
+        return pl.ds(first, count)
 
     def gather_copies(nb, ss, rs):
-        def c(k, img, half, to):
-            ref = nb.at[img, H[half], :]
+        def c(k, img, first, count, to):
+            ref = nb.at[img, rows_at(first, count), :]
             return rc(ref, ref, ss.at[k], rs.at[k], {"tensor": to})
 
-        send = [
-            c(0, me, 0, right), c(1, me, 1, left), c(2, me, 1, right), c(3, me, 0, left),
-            c(4, left, 0, right), c(5, right, 1, left),
-        ]
-        recv = [
-            c(0, left, 0, right), c(1, right, 1, left), c(2, left, 1, right), c(3, right, 0, left),
-            c(4, opp, 0, right), c(5, opp, 1, left),
-        ]
+        send, recv = [], []
+        for k, first in ((0, 0), (2, HALF)):
+            send += [c(k, me, first, HALF, right), c(k + 1, me, first, HALF, left)]
+            recv += [c(k, left, first, HALF, right), c(k + 1, right, first, HALF, left)]
+        for k, first in ((4, 0), (6, HALF)):
+            send += [c(k, left, first, QUART, right), c(k + 1, right, first + QUART, QUART, left)]
+            recv += [c(k, opp, first, QUART, right), c(k + 1, opp, first + QUART, QUART, left)]
         return send, recv
 
-    def gather_steps(s, send, recv):
-        @pl.when(s == 1)
-        def _():
-            recv[0].wait_recv()
-            send[4].start()
-            recv[1].wait_recv()
-            send[5].start()
-
-        @pl.when(s == 2)
-        def _():
-            recv[2].wait_recv()
-            recv[3].wait_recv()
-
-        @pl.when(s == 3)
-        def _():
-            recv[4].wait_recv()
-            recv[5].wait_recv()
+    def pass_on(b, send, recv):
+        for i in (0, 1):
+            recv[2 * b + i].wait_recv()
+            send[4 + 2 * b + i].start()
 
     def blocks(s):
         ia = lax.rem(me + pick(s, (0, 3, 3, 2)), NX)
         ib = lax.rem(me + pick(s, (0, 1, 1, 2)), NX)
         ha = pick(s, (0, 0, 1, 0))
-        hb = pick(s, (1, 1, 0, 1))
+        hb = pick(s, (1, 0, 1, 1))
         ra = pl.ds(pl.multiple_of(ha * HALF, HALF), HALF)
         rb = pl.ds(pl.multiple_of(hb * HALF, HALF), HALF)
         return ia, ra, ib, rb
 
     send2, recv2 = gather_copies(nb2, g2s, g2r)
-    for k in range(4):
-        send2[k].start()
-    step(3, 4)
-    step(2, 6)
-
-    def part_copy(s, k, img, src_img, dst_rows):
-        i = (s - 1) * 2 + k
-        return rc(
-            pbuf.at[s, H[k], :], precv.at[src_img, dst_rows, :], rss.at[i], rsr.at[i], {"tensor": img}
-        )
+    for b in (0, 1):
+        lax.fori_loop(2 * b, 2 * b + 2, second_norm, 0)
+        send2[2 * b].start()
+        send2[2 * b + 1].start()
+    step(1, 5)
+    step(1, 6)
+
+    def part(k, src, dst, to):
+        return rc(src, dst, rss.at[k], rsr.at[k], {"tensor": to})
+
+    def partial_copies(b):
+        f = b * HALF
+        mine = pbuf.at[1 + b]
+        far = pbuf.at[3]
+        low, high = rows_at(f, QUART), rows_at(f + QUART, QUART)
+        k = 6 * b
+        send = [
+            part(k, mine.at[rows_at(HALF + QUART, QUART), :], precv.at[0, high, :], right),
+            part(k + 1, mine.at[rows_at(0, QUART), :], precv.at[1, low, :], left),
+            part(k + 2, far.at[low, :], pacc.at[0, rows_at(b * QUART, QUART), :], right),
+            part(k + 3, far.at[high, :], pacc.at[1, rows_at(b * QUART, QUART), :], left),
+            part(k + 4, mine.at[rows_at(HALF, QUART), :], precv.at[0, low, :], right),
+            part(k + 5, mine.at[rows_at(QUART, QUART), :], precv.at[1, high, :], left),
+        ]
+        return send
+
+    parts = [partial_copies(b) for b in (0, 1)]
 
     def feed_forward(s, carry):
-        gather_steps(s, send2, recv2)
+        @pl.when(s == 2)
+        def _():
+            pass_on(1, send2, recv2)
+            parts[0][0].start()
+            parts[0][1].start()
+
+        @pl.when(s == 3)
+        def _():
+            for k in range(4, 8):
+                recv2[k].wait_recv()
+
         ia, ra, ib, rb = blocks(s)
 
         def widen(n, c):
@@ -469,8 +541,9 @@
 
         @pl.when(s == 0)
         def _():
-            step(3, 5)
-            step(3, 6)
+            pass_on(0, send2, recv2)
+            step(2, 5)
+            step(2, 6)
 
         def narrow(z, c):
             cols = pl.ds(pl.multiple_of(z * LW, 128), LW)
@@ -479,22 +552,29 @@
 
         lax.fori_loop(0, 4, narrow, 0)
 
-        @pl.when(s >= 1)
-        def _():
-            part_copy(s, 0, ia, me, ra).start()
-            part_copy(s, 1, ib, me, rb).start()
+        @pl.when(s == 2)
+        def _():
+            parts[1][0].start()
+            parts[1][1].start()
 
         return carry
 
     lax.fori_loop(0, 4, feed_forward, 0)
-
-    part_recvs = [
-        (1, 0, right, 0), (1, 1, left, 1), (2, 0, right, 1), (2, 1, left, 0), (3, 0, opp, 0), (3, 1, opp, 1),
-    ]
-    for s, k, src, half in part_recvs:
-        part_copy(s, k, src, src, H[half]).wait_recv()
+    for b in (0, 1):
+        parts[b][2].start()
+        parts[b][3].start()
     load(10).wait()
     load(11).wait()
+
+    for b in (0, 1):
+        came = rows_at(b * QUART, QUART)
+        for side, first in ((0, HALF), (1, QUART)):
+            parts[b][2 + side].wait_recv()
+            rows = rows_at(first, QUART)
+            pbuf[1 + b, rows, :] = (
+                pbuf[1 + b, rows, :].astype(F32) + pacc[side, came, :].astype(F32)
+            ).astype(BF)
+            parts[b][4 + side].start()
 
     gamma2 = fac[1, pl.ds(me, 1), :]
     scale3 = fin[me, 0:1, :]
@@ -502,16 +582,19 @@
 
     def third_norm(m, c):
         r = pl.ds(pl.multiple_of(m * 64, 64), 64)
-        mixed = pbuf[0, r, :].astype(F32) + precv[left, r, :].astype(F32)
-        mixed = mixed + precv[right, r, :].astype(F32) + precv[opp, r, :].astype(F32)
+        mixed = pbuf[0, r, :].astype(F32) + precv[0, r, :].astype(F32) + precv[1, r, :].astype(F32)
         nb3[me, r, :] = modulated(st[r, :] + gamma2 * mixed, scale3, shift3)
         return c
 
-    lax.fori_loop(0, 4, third_norm, 0)
-
     send3, recv3 = gather_copies(nb3, g3s, g3r)
-    for k in range(4):
-        send3[k].start()
+    for b in (0, 1):
+        for k in (0, 1, 4, 5):
+            parts[b][k].wait_recv()
+        lax.fori_loop(2 * b, 2 * b + 2, third_norm, 0)
+        send3[2 * b].start()
+        send3[2 * b + 1].start()
+
+    H = (rows_at(0, HALF), rows_at(HALF, HALF))
 
     def out_copy(s, k, img, rows):
         return pltpu.make_async_copy(
@@ -519,7 +602,19 @@
         )
 
     def head(s, carry):
-        gather_steps(s, send3, recv3)
+        @pl.when(s == 1)
+        def _():
+            pass_on(0, send3, recv3)
+
+        @pl.when(s == 2)
+        def _():
+            pass_on(1, send3, recv3)
+
+        @pl.when(s == 3)
+        def _():
+            for k in range(4, 8):
+                recv3[k].wait_recv()
+
         ia, ra, ib, rb = blocks(s)
 
         def tile(n, c):
@@ -535,7 +630,11 @@
 
     lax.fori_loop(0, 4, head, 0)
 
-    for r in range(4):
+    for v in (0, 1):
+        send, _ = qkv_copies(v)
+        for c in send:
+            c().wait_send()
+    for r in range(3):
         for v in (0, 1):
             send, _ = unit_copies(r, v)
             for k in range(9):
@@ -544,11 +643,12 @@
         c.wait_send()
     for jj in range(3):
         att_copy(jj, me, opp).wait_send()
-    for k in range(6):
+    for k in range(8):
         send2[k].wait_send()
         send3[k].wait_send()
-    for s, k, src, half in part_recvs:
-        part_copy(s, k, src, src, H[half]).wait_send()
+    for b in (0, 1):
+        for c in parts[b]:
+            c.wait_send()
     out_canvas.wait()
 
     def out_done(s, carry):
@@ -630,11 +730,12 @@
         vm((NX, TOK, LW), BF),
         vm((TOK, D), BF),
         vm((NX, TOK, D), BF),
-        vm((NX, TOK, D), BF),
+        vm((2, TOK, D), BF),
+        vm((2, HALF, D), BF),
         vm((NX, TOK, VL), BF),
         dma((13,)), dma((4,)), dma((8,)), dma((1,)),
-        dma((8, 9)), dma((8, 9)), dma((3,)), dma((3,)), dma((3,)), dma((3,)),
-        dma((6,)), dma((6,)), dma((6,)), dma((6,)), dma((6,)), dma((6,)),
+        dma((2, 20)), dma((2, 20)), dma((6, 9)), dma((6, 9)), dma((3,)), dma((3,)), dma((3,)), dma((3,)),
+        dma((8,)), dma((8,)), dma((12,)), dma((12,)), dma((8,)), dma((8,)),
     ]
     logits, canvas = pl.pallas_call(
         body,

time: 158 us -> 145 us (0.918)
  the two profiles are of different devices: /device:TPU:8 before, /device:TPU:1 now
where the time goes in v2:
time: 145 us
  Pallas kernels  141 us (97%)
  local copies, waits for them, and re-layouts  3.77 us (3%)
    pallas_call x1, Pallas kernels, local(): pl.pallas_call(body, out_shape=(jax.ShapeDtypeStruct((IMGS, TOK, VL), BF)...  141 us
    unnamed x4, local copies, waits for them, and re-layouts  3.77 us

profile of v2, /device:TPU:1, one launch (start us, length us, event | category | flops | bytes accessed | tf_op | source)
XLA Modules:
  0.0 145.3 jit_solution(14423962117907310766)
XLA Ops:
  0.6 140.9 %shard_map.167 = (bf16[4,256,1024]{2,1,0:T(8,128)(2,1)}, f32[4,32,256]{2,1,0:T(8,128)}) custom-call(s32[4,169]{1,0:T(4,128)} %tok_h.1, f32[32,4096]{1,0:T(8,128)} %bitcast.20, f32[4,32,256]{2,1,0:T(8,128)} %bitcast.24, f32[32,1536]{1,0:T(8,128)} %lift_h.1, f32[256,1536]{1,0:T(8,128)} %loc_h.1, f32[6,4,1536]{2,1,0:T(4,128)} %bitcast.21, f32[1,4]{1,0:T(1,128)} %sharp_s.1, ...), custom_call_target="tpu_custom_call" | custom-call | tf_op jit(solution)/shard_map/pallas_call | solution.py:740
  141.5 0.0 copy-start
  141.5 3.1 %copy.20 = bf16[4,256,1024]{2,1,0:T(8,128)(2,1)} copy(bf16[4,256,1024]{2,1,0:T(8,128)(2,1)} %get-tuple-element.8) | data formatting | bytes 4194304
  144.6 0.0 copy-done
  144.6 0.7 copy.21
Async XLA Ops:
  141.5 3.1 %copy-start = (f32[4,32,256]{2,1,0:T(8,128)S(1)}, f32[4,32,256]{2,1,0:T(8,128)}, u32[]{:S(2)}) copy-start(f32[4,32,256]{2,1,0:T(8,128)} %get-tuple-element.5) | copy-start | bytes 393220

commit v3 on v2

--- a/solution.py
+++ b/solution.py
@@ -64,11 +64,11 @@
 def body(
     tok_h, quant_h, canvas_h, lift_h, loc_h, fac_h, sharp_s, qkv_h, wo_h, up_h, wd_h,
     kc_h, vc_h, fin_h, voc_h, kron_h,
-    logits_h, canvas_o,
+    logits_o, canvas_o,
     tok, quant, canv, lift, loc, fac, kc, vc, fin, voc, kron,
     wq, wo, wu, wd,
-    emb, cout, st, nb1, nb2, nb3, qn, kn, vn, knc, att, attr, hid, pbuf, precv, pacc, lout,
-    load_sem, own_sem, out_sem, cout_sem,
+    emb, st, nb1, nb2, nb3, qn, kn, vn, knc, att, attr, hid, pbuf, precv, pacc,
+    load_sem, own_sem,
     qs, qr, us, ur, wos, wor, ats, atr, g2s, g2r, rss, rsr, g3s, g3r,
 ):
     me = lax.axis_index("tensor")
@@ -117,7 +117,8 @@
 
     barrier = pltpu.get_barrier_semaphore()
     peers = [{"tensor": right}, {"tensor": left}, {"tensor": opp}]
-    peers += [dpi(mz, yp, mc), dpi(mz, ym, mc), dpi(zp, my, mc), dpi(zm, my, mc), dpi(mz, my, 1 - mc)]
+    peers += [dpi(mz, yp, mc), dpi(mz, ym, mc), dpi(mz, yo, mc), dpi(zp, my, mc), dpi(zm, my, mc)]
+    peers += [dpi(zo, my, mc), dpi(mz, my, 1 - mc)]
     for dev in peers:
         pl.semaphore_signal(barrier, inc=1, device_id=dev, device_id_type=MESH)
     pl.semaphore_wait(barrier, len(peers))
@@ -152,8 +153,8 @@
         send = [
             (at(a, b, c0, c1), dev(ap, b)),
             (at(a, b, c0, c1), dev(am, b)),
-            (at(am, b, c0, ch), dev(ap, b)),
-            (at(ap, b, ch, c1), dev(am, b)),
+            (at(a, b, c0, ch), dev(ao, b)),
+            (at(a, b, ch, c1), dev(ao, b)),
         ]
         recv = [at(am, b, c0, c1), at(ap, b, c0, c1), at(ao, b, c0, ch), at(ao, b, ch, c1)]
         send += [(at(ai, b, c0, c1), dev(a, bp)) for ai in row]
@@ -171,8 +172,8 @@
         )
 
     QKV_STAGES = (
-        (((), (0, 1, 4, 8)),),
-        (((0,), (2, 5, 9)), ((1,), (3, 6, 10))),
+        (((), (0, 1, 2, 3, 4, 8)),),
+        (((0,), (5, 9)), ((1,), (6, 10))),
         (((2, 3), (7, 11, 16)),),
         (((4,), (12,)), ((5,), (13,)), ((10,), (14,))),
         (((11,), (15,)), ((6, 7), (17,)), ((8, 9), (18,))),
@@ -246,6 +247,8 @@
 
     load(6).wait()
     load(7).wait()
+    own_u.wait()
+    step(1, 1)
 
     def wo_copy(k, owner, to):
         part = wo.at[mz, my, mc, :, pl.ds(pl.multiple_of(owner * LW, 128), LW)]
@@ -275,11 +278,12 @@
 
     lax.fori_loop(0, 5, embed, 0)
     qkv_stage(1)
-    own_u.wait()
-    step(1, 1)
+    step(2, 1)
     lax.fori_loop(5, 8, embed, 0)
     qkv_stage(2)
-    step(2, 1)
+    for c in wo_recvs:
+        c.wait_recv()
+    step(0, 1)
 
     def modulated(rows_value, scale, shift):
         center = rows_value - jnp.mean(rows_value, axis=-1, keepdims=True)
@@ -299,7 +303,7 @@
             precision=lax.Precision.HIGHEST, preferred_element_type=F32,
         )
         can = canv[j] + lifted
-        cout[j] = can
+        canvas_o[j] = can
         can_hi, can_lo = high_low(can)
         can3 = jnp.concatenate([can_hi, can_lo, can_hi], axis=0)
         for n in range(3):
@@ -322,30 +326,25 @@
         @pl.when(jj == 0)
         def _():
             qkv_stage(3)
-            for c in wo_recvs:
-                c.wait_recv()
-            step(0, 1)
+            step(0, 2)
 
         @pl.when(jj == 1)
         def _():
             qkv_stage(4)
-            step(0, 2)
+            step(1, 2)
+            step(0, 3)
 
         @pl.when(jj == 2)
         def _():
-            step(1, 2)
+            step(2, 2)
 
         @pl.when(jj == 3)
         def _():
             qkv_stage(5)
-            step(0, 3)
-            step(2, 2)
 
         return carry
 
     lax.fori_loop(0, 4, first_norm, 0)
-    out_canvas = pltpu.make_async_copy(cout, canvas_o, cout_sem.at[0])
-    out_canvas.start()
 
     load(8).wait()
     load(9).wait()
@@ -375,7 +374,6 @@
 
     lax.fori_loop(0, 4, cache_keys, 0)
     qkv_stage(6)
-    step(1, 3)
 
     def att_copy(jj, owner, to):
         return rc(att.at[jj], attr.at[owner], ats.at[jj], atr.at[jj], {"tensor": to})
@@ -389,6 +387,20 @@
         k = dot(x, wq[:, :, :, :, LW : 2 * LW].reshape(D, LW))
         kn[...] = unit(k).astype(BF)
         vn[...] = dot(x, wq[:, :, :, :, 2 * LW : 3 * LW].reshape(D, LW)).astype(BF)
+        @pl.when(jj == 0)
+        def _():
+            step(0, 4)
+            step(1, 3)
+
+        @pl.when(jj == 1)
+        def _():
+            step(2, 3)
+
+        @pl.when(jj == 2)
+        def _():
+            step(0, 5)
+
+        outs = []
         for h in range(HEADS_L):
             w0, w1 = WINDOWS[h]
             lanes = lax.broadcasted_iota(jnp.int32, (TOK, w1 - w0), 1) + w0
@@ -403,23 +415,14 @@
             pn = jnp.exp(sn - top)
             total = jnp.sum(pc, axis=-1, keepdims=True) + jnp.sum(pn, axis=-1, keepdims=True)
             o = dot(pc.astype(BF), vc[j, :, w0:w1]) + dot(pn.astype(BF), vn[:, w0:w1])
-            o = (o * (1.0 / total)).astype(BF)
-            if h == 0:
-                att[jj, :, w0:w1] = o
-            else:
-                att[jj, :, w0:w1] = jnp.where(mine, o, att[jj, :, w0:w1])
-
-        @pl.when(jj == 0)
-        def _():
-            step(0, 4)
-
-        @pl.when(jj == 1)
-        def _():
-            step(2, 3)
-
-        @pl.when(jj == 2)
-        def _():
-            step(1, 4)
+            outs.append(o * (1.0 / total))
+        lane = lax.broadcasted_iota(jnp.int32, (TOK, 128), 1)
+        for c in range(3):
+            w0 = WINDOWS[c + 1][0]
+            first = outs[c][:, c * 128 - WINDOWS[c][0] : c * 128 - WINDOWS[c][0] + 128]
+            second = outs[c + 1][:, c * 128 - w0 : c * 128 - w0 + 128]
+            edge = (c + 1) * HDIM - c * 128
+            att[jj, :, c * 128 : (c + 1) * 128] = jnp.where(lane < edge, first, second).astype(BF)
 
         @pl.when(jj < 3)
         def _():
@@ -427,14 +430,12 @@
 
         return carry
 
-    att[...] = jnp.zeros_like(att)
     lax.fori_loop(0, 4, attend, 0)
     attr[me] = att[3]
-    step(0, 5)
     for jj in range(3):
         att_copy(jj, lax.rem(me + 4 - ORDER[jj], NX), opp).wait_recv()
-    step(2, 4)
     step(0, 6)
+    step(1, 4)
 
     def mix(z, carry):
         cols = pl.ds(pl.multiple_of(z * LW, 128), LW)
@@ -491,8 +492,8 @@
         lax.fori_loop(2 * b, 2 * b + 2, second_norm, 0)
         send2[2 * b].start()
         send2[2 * b + 1].start()
+    step(2, 4)
     step(1, 5)
-    step(1, 6)
 
     def part(k, src, dst, to):
         return rc(src, dst, rss.at[k], rsr.at[k], {"tensor": to})
@@ -515,54 +516,72 @@
 
     parts = [partial_copies(b) for b in (0, 1)]
 
-    def feed_forward(s, carry):
-        @pl.when(s == 2)
-        def _():
-            pass_on(1, send2, recv2)
-            parts[0][0].start()
-            parts[0][1].start()
-
-        @pl.when(s == 3)
-        def _():
-            for k in range(4, 8):
-                recv2[k].wait_recv()
-
+    def widen(s):
         ia, ra, ib, rb = blocks(s)
 
-        def widen(n, c):
+        def tile(n, c):
             cols = pl.ds(pl.multiple_of(n * LW, 128), LW)
             x = jnp.concatenate([nb2[ia, ra, :], nb2[ib, rb, :]], axis=0)
             u = dot(x, wu[:, :, :, :, cols].reshape(D, LW))
             act = 0.5 * u * (1.0 + jnp.tanh(0.7978845608028654 * (u + 0.044715 * (u * u * u))))
-            hid[:, cols] = act.astype(BF)
+            hid[s, :, cols] = act.astype(BF)
             return c
 
-        lax.fori_loop(0, 4, widen, 0)
-
-        @pl.when(s == 0)
-        def _():
-            pass_on(0, send2, recv2)
+        lax.fori_loop(0, 4, tile, 0)
+
+    def narrow(s):
+        def tile(z, c):
+            cols = pl.ds(pl.multiple_of(z * LW, 128), LW)
+            pbuf[s, :, cols] = dot_nt(hid[s], wd[z].reshape(LW, D)).astype(BF)
+            return c
+
+        lax.fori_loop(0, 4, tile, 0)
+
+    pass_on(0, send2, recv2)
+    step(1, 6)
+
+    def widen_ready(t, carry):
+        s = pick(t, (1, 0, 2, 3))
+
+        @pl.when(t == 1)
+        def _():
             step(2, 5)
+
+        @pl.when(t == 2)
+        def _():
+            pass_on(1, send2, recv2)
+
+        @pl.when(t == 3)
+        def _():
             step(2, 6)
 
-        def narrow(z, c):
-            cols = pl.ds(pl.multiple_of(z * LW, 128), LW)
-            pbuf[s, :, cols] = dot_nt(hid[...], wd[z].reshape(LW, D)).astype(BF)
-            return c
-
-        lax.fori_loop(0, 4, narrow, 0)
-
-        @pl.when(s == 2)
-        def _():
-            parts[1][0].start()
-            parts[1][1].start()
-
+            def near(s, c):
+                narrow(s)
+                return c
+
+            lax.fori_loop(1, 3, near, 0)
+            for b in (0, 1):
+                parts[b][0].start()
+                parts[b][1].start()
+            for k in range(4, 8):
+                recv2[k].wait_recv()
+
+        widen(s)
         return carry
 
-    lax.fori_loop(0, 4, feed_forward, 0)
-    for b in (0, 1):
-        parts[b][2].start()
-        parts[b][3].start()
+    lax.fori_loop(0, 4, widen_ready, 0)
+
+    def narrow_last(t, carry):
+        @pl.when(t == 1)
+        def _():
+            for b in (0, 1):
+                parts[b][2].start()
+                parts[b][3].start()
+
+        narrow(pick(t, (3, 0)))
+        return carry
+
+    lax.fori_loop(0, 2, narrow_last, 0)
     load(10).wait()
     load(11).wait()
 
@@ -594,13 +613,6 @@
         send3[2 * b].start()
         send3[2 * b + 1].start()
 
-    H = (rows_at(0, HALF), rows_at(HALF, HALF))
-
-    def out_copy(s, k, img, rows):
-        return pltpu.make_async_copy(
-            lout.at[s, H[k], :], logits_h.at[img, rows, :], out_sem.at[2 * s + k]
-        )
-
     def head(s, carry):
         @pl.when(s == 1)
         def _():
@@ -620,12 +632,12 @@
         def tile(n, c):
             cols = pl.ds(pl.multiple_of(n * 256, 256), 256)
             x = jnp.concatenate([nb3[ia, ra, :], nb3[ib, rb, :]], axis=0)
-            lout[s, :, cols] = dot(x, voc[:, cols]).astype(BF)
+            y = dot(x, voc[:, cols]).astype(BF)
+            logits_o[ia, ra, cols] = y[:HALF]
+            logits_o[ib, rb, cols] = y[HALF:]
             return c
 
         lax.fori_loop(0, 4, tile, 0)
-        out_copy(s, 0, ia, ra).start()
-        out_copy(s, 1, ib, rb).start()
         return carry
 
     lax.fori_loop(0, 4, head, 0)
@@ -649,15 +661,6 @@
     for b in (0, 1):
         for c in parts[b]:
             c.wait_send()
-    out_canvas.wait()
-
-    def out_done(s, carry):
-        ia, ra, ib, rb = blocks(s)
-        out_copy(s, 0, ia, ra).wait()
-        out_copy(s, 1, ib, rb).wait()
-        return carry
-
-    lax.fori_loop(0, 4, out_done, 0)
 
 
 def local(
@@ -717,7 +720,6 @@
         vm((4, 4, 2, SH, D), BF),
         vm((4, 4, 2, SH, D), BF),
         vm((IMGS, 2 * CVAE, PREVTOK), F32),
-        vm((IMGS, CVAE, TOK), F32),
         vm((TOK, D), F32),
         vm((IMGS, TOK, D), BF),
         vm((IMGS, TOK, D), BF),
@@ -728,26 +730,25 @@
         vm((IMGS, CACHE, LW), BF),
         vm((NX, TOK, LW), BF),
         vm((NX, TOK, LW), BF),
-        vm((TOK, D), BF),
+        vm((NX, TOK, D), BF),
         vm((NX, TOK, D), BF),
         vm((2, TOK, D), BF),
         vm((2, HALF, D), BF),
-        vm((NX, TOK, VL), BF),
-        dma((13,)), dma((4,)), dma((8,)), dma((1,)),
+        dma((13,)), dma((4,)),
         dma((2, 20)), dma((2, 20)), dma((6, 9)), dma((6, 9)), dma((3,)), dma((3,)), dma((3,)), dma((3,)),
         dma((8,)), dma((8,)), dma((12,)), dma((12,)), dma((8,)), dma((8,)),
     ]
     logits, canvas = pl.pallas_call(
         body,
         out_shape=(
-            jax.ShapeDtypeStruct((IMGS, TOK, VL), BF),
-            jax.ShapeDtypeStruct((IMGS, CVAE, TOK), F32),
+            pltpu.VMEM((IMGS, TOK, VL), BF),
+            pltpu.VMEM((IMGS, CVAE, TOK), F32),
         ),
         in_specs=specs,
-        out_specs=(anyspace, anyspace),
+        out_specs=(pl.BlockSpec(memory_space=pltpu.VMEM), pl.BlockSpec(memory_space=pltpu.VMEM)),
         scratch_shapes=scratch,
         compiler_params=pltpu.CompilerParams(
-            collective_id=0, has_side_effects=True, vmem_limit_bytes=67_000_000
+            collective_id=0, has_side_effects=True, vmem_limit_bytes=60_000_000
         ),
     )(*operands)
     return logits, jnp.swapaxes(canvas, 1, 2)

time: 145 us -> 135 us (0.931)
  the two profiles are of different devices: /device:TPU:1 before, /device:TPU:8 now
where the time goes in v3:
time: 135 us
  Pallas kernels  132 us (98%)
  local copies, waits for them, and re-layouts  1.98 us (1%)
    pallas_call x1, Pallas kernels, local(): pl.pallas_call(body, out_shape=(pltpu.VMEM((IMGS, TOK, VL), BF), pltpu.VM...  132 us

profile of v3, /device:TPU:8, one launch (start us, length us, event | category | flops | bytes accessed | tf_op | source)
XLA Modules:
  0.0 134.5 jit_solution(412243092145575252)
XLA Ops:
  0.6 131.9 %shard_map.167 = (bf16[4,256,1024]{2,1,0:T(8,128)(2,1)S(1)}, f32[4,32,256]{2,1,0:T(8,128)S(1)}) custom-call(s32[4,169]{1,0:T(4,128)} %tok_h.1, f32[32,4096]{1,0:T(8,128)} %bitcast.21, f32[4,32,256]{2,1,0:T(8,128)} %bitcast.25, f32[32,1536]{1,0:T(8,128)} %lift_h.1, f32[256,1536]{1,0:T(8,128)} %loc_h.1, f32[6,4,1536]{2,1,0:T(4,128)} %bitcast.22, ...), custom_call_target="tpu_custom_call" | custom-call | tf_op jit(solution)/shard_map/pallas_call | solution.py:741
  132.5 1.3 copy.20
  133.9 0.7 copy.21

commit v4 on v3

--- a/solution.py
+++ b/solution.py
@@ -622,11 +622,6 @@
         def _():
             pass_on(1, send3, recv3)
 
-        @pl.when(s == 3)
-        def _():
-            for k in range(4, 8):
-                recv3[k].wait_recv()
-
         ia, ra, ib, rb = blocks(s)
 
         def tile(n, c):
@@ -640,7 +635,18 @@
         lax.fori_loop(0, 4, tile, 0)
         return carry
 
-    lax.fori_loop(0, 4, head, 0)
+    lax.fori_loop(0, 3, head, 0)
+    for b in (0, 1):
+        recv3[4 + 2 * b].wait_recv()
+        recv3[5 + 2 * b].wait_recv()
+        rows = rows_at(b * HALF, HALF)
+
+        def last_tile(n, c):
+            cols = pl.ds(pl.multiple_of(n * 256, 256), 256)
+            logits_o[opp, rows, cols] = dot(nb3[opp, rows, :], voc[:, cols]).astype(BF)
+            return c
+
+        lax.fori_loop(0, 4, last_tile, 0)
 
     for v in (0, 1):
         send, _ = qkv_copies(v)

time: 135 us -> 135 us (level)
  no operation moved by 1% of the time
where the time goes in v4:
time: 135 us; the launch traced here: 134 us
  Pallas kernels  132 us (98%)
  local copies, waits for them, and re-layouts  1.98 us (1%)
    pallas_call x1, Pallas kernels, local(): pl.pallas_call(body, out_shape=(pltpu.VMEM((IMGS, TOK, VL), BF), pltpu.VM...  132 us

profile of v4, /device:TPU:8, one launch (start us, length us, event | category | flops | bytes accessed | tf_op | source)
XLA Modules:
  0.0 134.1 jit_solution(13054767104337427112)
XLA Ops:
  0.6 131.5 %shard_map.167 = (bf16[4,256,1024]{2,1,0:T(8,128)(2,1)S(1)}, f32[4,32,256]{2,1,0:T(8,128)S(1)}) custom-call(s32[4,169]{1,0:T(4,128)} %tok_h.1, f32[32,4096]{1,0:T(8,128)} %bitcast.21, f32[4,32,256]{2,1,0:T(8,128)} %bitcast.25, f32[32,1536]{1,0:T(8,128)} %lift_h.1, f32[256,1536]{1,0:T(8,128)} %loc_h.1, f32[6,4,1536]{2,1,0:T(4,128)} %bitcast.22, ...), custom_call_target="tpu_custom_call" | custom-call | tf_op jit(solution)/shard_map/pallas_call | solution.py:747
  132.1 1.3 copy.20
  133.5 0.7 copy.21
